TPU v7x, 32 devices: a 4x4x1 block of a 4x4x8 slice. The times are simulated.
32 devices in a mesh: data: 1 (over z), model: 4 (over y), seq: 8 (over x, core).
Axes of the slice: x: 4, y: 4, z: 1, core: 2. Of those that a mesh axis runs over, the one named last changes fastest.
The devices are a block of a 4x4x8 slice.
Arguments:
- tokens: bfloat16 [64, 4096, 768], P('data', 'seq')
- lengths: int32 [64], P('data')
- slot_params: bfloat16 [768, 128], replicated
- logit_scale: float32 [], replicated
- w_in: bfloat16 [32, 768, 3072], P('seq', None, 'model')
- w_out: bfloat16 [32, 3072, 768], P('seq', 'model')
Outputs:
- output: bfloat16 [64, 4096, 768], P('data', 'seq')
All inputs are finite; a program needn't handle non-finite values.
Results may differ from a plain program's by a relative error of at most 0.0153139.
Values are sent between devices in bfloat16 or wider.
A program may use at most 768 MiB of HBM per device.

v0:
```python
import jax
import jax.numpy as jnp
from jax import lax
from jax.sharding import PartitionSpec as P

NORM_EPS = 1e-6


def unit_vectors(values, axis):
    v32 = values.astype(jnp.float32)
    return (v32 * lax.rsqrt(jnp.sum(v32 * v32, axis=axis, keepdims=True) + NORM_EPS)).astype(jnp.bfloat16)


def solution(mesh):
    seq_size = mesh.shape["seq"]

    def local_layer(tokens, lengths, slot_params, logit_scale, w_in, w_out):
        batch_size, tok_count, model_dim = tokens.shape
        n_slots = slot_params.shape[1]
        local_experts = w_in.shape[0]
        local_slots = n_slots // seq_size
        slot_per = local_slots // local_experts
        positions = lax.axis_index("seq") * tok_count + jnp.arange(tok_count)
        is_valid = positions[None, :] < lengths[:, None]
        logits = logit_scale * jnp.einsum("bmd,dn->bmn", unit_vectors(tokens, 2), unit_vectors(slot_params, 0), preferred_element_type=jnp.float32)
        masked = jnp.where(is_valid[:, :, None], logits, -1e30)
        col_max = lax.pmax(jnp.max(masked, axis=1, keepdims=True), "seq")
        weights = jnp.exp(masked - col_max)
        col_sum = lax.psum_scatter(jnp.sum(weights, axis=1), "seq", scatter_dimension=1, tiled=True)
        part_sum = jnp.einsum("bmn,bmd->bnd", weights.astype(jnp.bfloat16), tokens, preferred_element_type=jnp.float32)
        slot_sum = lax.psum_scatter(part_sum.astype(jnp.bfloat16), "seq", scatter_dimension=1, tiled=True)
        slot_in = (slot_sum.astype(jnp.float32) / col_sum[:, :, None]).astype(jnp.bfloat16)
        grouped = slot_in.reshape(batch_size, local_experts, slot_per, model_dim)
        hidden = jnp.einsum("besd,edf->besf", grouped, w_in, preferred_element_type=jnp.float32)
        hidden = jax.nn.gelu(hidden, approximate=False).astype(jnp.bfloat16)
        out_part = jnp.einsum("besf,efd->besd", hidden, w_out, preferred_element_type=jnp.float32)
        slot_out = lax.psum(out_part, "model").astype(jnp.bfloat16).reshape(batch_size, local_slots, model_dim)
        all_slots = lax.all_gather(slot_out, "seq", axis=1, tiled=True)
        mix_weights = jax.nn.softmax(logits, axis=-1).astype(jnp.bfloat16)
        mixed = jnp.einsum("bmn,bnd->bmd", mix_weights, all_slots, preferred_element_type=jnp.float32)
        return jnp.where(is_valid[:, :, None], mixed, 0.0).astype(jnp.bfloat16)

    return jax.shard_map(local_layer, mesh=mesh, in_specs=(P("data", "seq", None), P("data"), P(), P(), P("seq", None, "model"), P("seq", "model", None)), out_specs=P("data", "seq", None), check_vma=False)
```

profile of v0, /device:TPU:97, one launch (start us, length us, event | category | flops | bytes accessed | tf_op | source)
XLA Modules:
  0.0 364.0 jit_solution(5458970490332446396)
XLA Ops:
  6.5 0.0 reduce-scatter.7.cloned.1.call-start
  7.2 1.0 fusion.82
  8.3 0.0 copy-start.1
  8.3 0.0 copy-start
  8.3 17.1 %fusion.1 = f32[64,512]{1,0:T(8,128)S(1)} fusion(bf16[64,512,768]{2,1,0:T(8,128)(2,1)} %param.6), kind=kLoop, calls=%fused_computation.3 | loop fusion | flops 75464704 | bytes 50462720 | tf_op jit(solution)/shard_map/reduce_sum | solution.py:11
  25.4 0.0 copy-done.1
  25.4 0.1 broadcast_compare_fusion
  25.5 0.0 copy-done
  25.5 23.7 %select_reduce_fusion = (f32[64,128]{1,0:T(8,128)S(1)}, f32[64,512,128]{2,1,0:T(8,128)}) fusion(f32[]{:T(128)S(6)} %copy.21, pred[64,512]{1,0:T(8,128)(4,1)S(1)} %broadcast_compare_fusion, bf16[768,128]{1,0:T(8,128)(2,1)S(1)} %copy-done, f32[128]{0:T(128)S(1)} %add_rsqrt_fusion.1, bf16[64,512,768]{2,1,0:T(8,128)(2,1)} %param.6, f32[64,512]{1,0:T(8,128)S(1)} %add_rsqrt_fusion), kind=kOutput, calls=%fused_computation.11 | convolution fusion | flops 6530818048 | bytes 67502592 | tf_op jit(solution)/shard_map/bmd,dn->bmn/dot_general | solution.py:25
  49.2 24.0 %pmax.7 = f32[64,128]{1,0:T(8,128)S(1)} all-reduce(f32[64,128]{1,0:T(8,128)S(1)} %get-tuple-element.5), channel_id=1, replica_groups=mesh['data'=1,'model'=4,'seq'=8] {'seq'}, use_global_device_ids=true, to_apply=%region_5.6 | all-reduce | flops 8192 | bytes 65536 | tf_op jit(solution)/shard_map/pmax | solution.py:27
  73.2 7.2 %fusion.6 = f32[64,128]{1,0:T(8,128)S(1)} fusion(f32[64,512,128]{2,1,0:T(8,128)} %get-tuple-element.6, f32[64,128]{1,0:T(8,128)S(1)} %pmax.7, f32[]{:T(128)S(6)} %copy.21, pred[64,512]{1,0:T(8,128)(4,1)S(1)} %broadcast_compare_fusion), kind=kLoop, calls=%fused_computation.12 | loop fusion | flops 16769024 | bytes 16875524 | tf_op jit(solution)/shard_map/reduce_sum | solution.py:29
  80.4 0.7 copy.17
  81.2 0.1 reduce-scatter.7.cloned.1.call-update
  81.2 0.1 reduce-scatter.5.cloned.1.call-start
  81.3 28.2 %fusion.19 = bf16[64,128,768]{2,1,0:T(8,128)(2,1)} fusion(bf16[64,512,768]{2,1,0:T(8,128)(2,1)} %param.6, f32[64,512,128]{2,1,0:T(8,128)} %get-tuple-element.6, f32[64,128]{1,0:T(8,128)S(1)} %pmax.7, f32[]{:T(128)S(6)} %copy.21, pred[64,512]{1,0:T(8,128)(4,1)S(1)} %broadcast_compare_fusion), kind=kOutput, calls=%fused_computation.23 | convolution fusion | flops 6465519616 | bytes 79757312 | tf_op jit(solution)/shard_map/bmn,bmd->bnd/dot_general | solution.py:30
  109.5 0.1 reduce-scatter.5.cloned.1.call-update
  109.5 0.1 all-gather.2.cloned.1.call-start
  109.6 0.1 reduce-scatter.7.cloned.1.call-done
  109.7 0.8 copy.18
  110.5 72.6 %reduce-scatter.5.cloned.1.call-done = bf16[64,16,768]{2,1,0:T(8,128)(2,1)} async-done(((bf16[64,128,768]{2,1,0:T(8,128)(2,1)}), bf16[64,16,768]{2,1,0:T(8,128)(2,1)}) %reduce-scatter.5.cloned.1.call-update) | async-done | bytes 1572880 | tf_op jit(solution)/shard_map/reduce_scatter | solution.py:31
  183.0 1.8 divide_convert_fusion.2
  184.8 0.5 copy.16
  185.3 12.5 %fusion.44 = f32[64,4,4,768]{3,0,2,1:T(8,128)} fusion(bf16[4,768,768]{2,1,0:T(8,128)(2,1)} %param.11, bf16[64,4,4,768]{3,0,2,1:T(8,128)(2,1)S(1)} %bitcast.101, bf16[4,768,768]{2,1,0:T(8,128)(2,1)} %param.10), kind=kOutput, calls=%fused_computation.53 | convolution fusion | flops 2467037184 | bytes 14155776 | tf_op jit(solution)/shard_map/besf,efd->besd/dot_general | solution.py:36
  197.8 59.1 %all-reduce.1 = bf16[64,4,4,768]{3,0,2,1:T(8,128)(2,1)S(1)} all-reduce(f32[64,4,4,768]{3,0,2,1:T(8,128)} %fusion.44), channel_id=1, replica_groups=mesh['data'=1,'model'=4,'seq'=8] {'model'}, use_global_device_ids=true, to_apply=%region_9.10 | all-reduce | flops 786432 | bytes 4718592 | tf_op jit(solution)/shard_map/psum | solution.py:37
  256.9 2.1 copy.12
  259.0 0.1 all-gather.2.cloned.1.call-update
  259.0 22.0 %fusion.118 = (f32[64,512]{1,0:T(8,128)S(1)}, f32[64,512,128]{2,1,0:T(8,128)}) fusion(f32[64,512,128]{2,1,0:T(8,128)} %get-tuple-element.6, f32[]{:T(128)S(6)} %copy.21), kind=kOutput, calls=%fused_computation.125 | output fusion | flops 16777344 | bytes 33685508 | tf_op jit(solution)/shard_map/sub | solution.py:39
  281.1 45.8 %all-gather.2.cloned.1.call-done = bf16[64,128,768]{2,1,0:T(8,128)(2,1)} async-done(((bf16[64,16,768]{2,1,0:T(8,128)(2,1)}), bf16[64,128,768]{2,1,0:T(8,128)(2,1)}) %all-gather.2.cloned.1.call-update) | async-done | bytes 12582928 | tf_op jit(solution)/shard_map/all_gather | solution.py:38
  326.9 30.6 %select_convert_fusion = bf16[64,512,768]{2,1,0:T(8,128)(2,1)} fusion(pred[64,512]{1,0:T(8,128)(4,1)S(1)} %broadcast_compare_fusion, bf16[64,128,768]{2,1,0:T(8,128)(2,1)} %all-gather.2.cloned.1.call-done, f32[64,512,128]{2,1,0:T(8,128)} %get-tuple-element.8, f32[64,512]{1,0:T(8,128)S(1)} %get-tuple-element.7), kind=kOutput, calls=%fused_computation.5 | convolution fusion | flops 6501171200 | bytes 79855616 | tf_op jit(solution)/shard_map/bmn,bnd->bmd/dot_general | solution.py:40
  (3 shorter events, 0.0 us)
Async XLA Ops:
  6.5 103.1 %reduce-scatter.7.cloned.1.call-start = ((), (), s32[]{:S(2)}) async-start(), calls=%async_computation.4 | async-start | bytes 73728
  8.3 17.1 %copy-start.1 = (s32[64]{0:T(128)S(1)}, s32[64]{0:T(128)}, u32[]{:S(2)}) copy-start(s32[64]{0:T(128)} %param.7) | copy-start | bytes 772
  8.3 17.2 %copy-start = (bf16[768,128]{1,0:T(8,128)(2,1)S(1)}, bf16[768,128]{1,0:T(8,128)(2,1)}, u32[]{:S(2)}) copy-start(bf16[768,128]{1,0:T(8,128)(2,1)} %param.8) | copy-start | bytes 589828
  81.2 101.8 %reduce-scatter.5.cloned.1.call-start = ((), (), s32[]{:S(2)}) async-start(), calls=%async_computation.2 | async-start | bytes 14155776 | tf_op jit(solution)/shard_map/reduce_scatter | solution.py:31
  109.5 217.3 %all-gather.2.cloned.1.call-start = ((), (), s32[]{:S(2)}) async-start(), calls=%async_computation.3 | async-start | bytes 14155776 | tf_op jit(solution)/shard_map/all_gather | solution.py:38
Sparse Core Ops, SparseCore 0:
  81.3 28.2 reduce-scatter.6
  112.0 70.9 reduce-scatter.4
  259.2 67.6 all-gather.1
where the time goes:
time: 364 us
  waiting for transfers between devices  119 us (33%)
  matrix products  95 us (26%)
  blocking collectives  83.1 us (23%)
  other arithmetic  49.3 us (14%)
  between operations  13.9 us (4%)
  local copies, waits for them, and re-layouts  4.03 us (1%)
    reduce_scatter x1, waiting for transfers between devices, local_layer(): lax.psum_scatter(part_sum.astype(jnp.bfloat16), 'seq', scatter_dimension=...  72.6 us
    psum x1, blocking collectives, local_layer(): lax.psum(out_part, 'model').astype(jnp.bfloat16)  59.1 us
    all_gather x1, waiting for transfers between devices, local_layer(): all_slots = lax.all_gather(slot_out, 'seq', axis=1, tiled=True)  45.8 us
    dot_general x1, matrix products, local_layer(): jnp.einsum('bmn,bnd->bmd', mix_weights, all_slots, preferred_element_type...  30.6 us
    dot_general x1, matrix products, local_layer(): jnp.einsum('bmn,bmd->bnd', weights.astype(jnp.bfloat16), tokens, preferre...  28.2 us
    pmax x1, blocking collectives, local_layer(): col_max = lax.pmax(jnp.max(masked, axis=1, keepdims=True), 'seq')  24 us
    dot_general x1, matrix products, local_layer(): jnp.einsum('bmd,dn->bmn', unit_vectors(tokens, 2), unit_vectors(slot_para...  23.7 us
    sub x1, other arithmetic, local_layer(): mix_weights = jax.nn.softmax(logits, axis=-1).astype(jnp.bfloat16)  22 us
  transfers between devices with their start and end apart: 3, of which 3 were waited for; matrix products, arithmetic and copies ran while one was open for 14% of the time, Pallas kernels for 0%

commit v1 on v0

v1 whole, which is shorter than its diff:
```python
import functools

import jax
import jax.numpy as jnp
import numpy as np
from jax import lax
from jax.experimental import pallas as pl
from jax.experimental.pallas import tpu as pltpu
from jax.sharding import PartitionSpec as P

NORM_EPS = 1e-6
NEG = -1e30
MESH = pl.DeviceIdType.MESH
CORES = 2
RING = 4
CHUNKS = 2
TOK_BUFS = 3
VMEM_LIMIT = 60 * 1024 * 1024


def unit_vectors(values, axis):
    v32 = values.astype(jnp.float32)
    return (v32 * lax.rsqrt(jnp.sum(v32 * v32, axis=axis, keepdims=True) + NORM_EPS)).astype(jnp.bfloat16)


def scaled_logits(x, v, g):
    return g * jnp.dot(unit_vectors(x, 1), v, preferred_element_type=jnp.float32)


def row_softmax(logits):
    e = jnp.exp(logits - jnp.max(logits, axis=1, keepdims=True))
    return (e * (1.0 / jnp.sum(e, axis=1, keepdims=True))).astype(jnp.bfloat16)


def dispatch_kernel(pos_ref, len_ref, g_ref, x_ref, v_ref, s_ref, mz_ref, c_ref):
    i = pl.program_id(0)
    group, toks = s_ref.shape[0], x_ref.shape[1]
    del group
    x = x_ref[0]
    logits = scaled_logits(x, v_ref[...], g_ref[0])
    c_ref[0] = row_softmax(logits)
    first = pos_ref[1] * toks
    length = len_ref[pos_ref[0] * pl.num_programs(0) + i]
    valid = first + lax.broadcasted_iota(jnp.int32, logits.shape, 0) < length
    masked = jnp.where(valid, logits, NEG)
    top = jnp.max(masked, axis=0, keepdims=True)
    w = jnp.where(valid, jnp.exp(masked - top), 0.0)
    mz_ref[0, pl.ds(i, 1), :] = top
    mz_ref[1, pl.ds(i, 1), :] = jnp.sum(w, axis=0, keepdims=True)
    s_ref[0] = lax.dot_general(w.astype(jnp.bfloat16), x, (((0,), (0,)), ((), ())), preferred_element_type=jnp.float32).astype(jnp.bfloat16)


def exchange_kernel(dims, plan, tok_hbm, g_ref, v_ref, s_hbm, mz_ref, win_hbm, wout_hbm, perm_ref, permt_ref,
                    ysa_hbm, ysb_hbm, c_hbm,
                    tokbuf, cbuf, s_buf, mz_all, win, wout, sc, dr, pb, fx, sx, rx, xs, op, fy, sy, ry, ysa, ysb,
                    tok_sem, c_sem, load_sem, out_sem, send_sem, recv_sem):
    chunks, bc, n_seq, group, n_fill, slots = dims
    bh, bq = bc // 2, bc // 4
    n = bc * slots
    m, s = lax.axis_index("model"), lax.axis_index("seq")
    c, x = lax.rem(s, CORES), lax.div(s, CORES)
    oc = 1 - c
    xr, xl, xo = lax.rem(x + 1, RING), lax.rem(x + RING - 1, RING), lax.rem(x + 2, RING)
    mr, ml, mo = lax.rem(m + 1, RING), lax.rem(m + RING - 1, RING), lax.rem(m + 2, RING)
    right, left = {"seq": xr * CORES + c}, {"seq": xl * CORES + c}
    up, down = {"model": mr}, {"model": ml}
    twin = {"seq": x * CORES + oc}
    row_peers = [{"seq": lax.rem(s + d, n_seq)} for d in range(1, n_seq)]
    peers = row_peers + [up, down]

    loads = [pltpu.make_async_copy(a, b, load_sem.at[i]) for i, (a, b) in enumerate(((s_hbm, s_buf), (win_hbm, win), (wout_hbm, wout)))]
    for ld in loads:
        ld.start()
    batch = tok_hbm.shape[0]

    def tok_copy(i):
        b = lax.rem((m + 1) * group + i, batch)
        slot = lax.rem(i, TOK_BUFS)
        return pltpu.make_async_copy(tok_hbm.at[b], tokbuf.at[slot], tok_sem.at[slot])

    def c_copy(i):
        slot = lax.rem(i, 2)
        return pltpu.make_async_copy(cbuf.at[slot], c_hbm.at[i], c_sem.at[slot])

    for i in range(TOK_BUFS - 1):
        tok_copy(jnp.int32(i)).start()

    barrier = pltpu.get_barrier_semaphore()
    for peer in peers:
        pl.semaphore_signal(barrier, inc=1, device_id=peer, device_id_type=MESH)
    pl.semaphore_wait(barrier, len(peers))

    copies = []

    def send(src, dst, dev):
        i = len(copies)
        d = pltpu.make_async_remote_copy(src_ref=src, dst_ref=dst, send_sem=send_sem.at[i], recv_sem=recv_sem.at[i], device_id=dev, device_id_type=MESH)
        d.start()
        copies.append(d)
        return d

    mz_sends = [send(mz_ref, mz_all.at[s], peer) for peer in row_peers]
    mz_all[s] = mz_ref[...]

    filled = [0]

    def fill(count):
        lo = filled[0]
        hi = min(lo + count, n_fill)
        filled[0] = hi
        if hi == lo:
            return

        def one(i, carry):
            tok_copy(i).wait()

            @pl.when(i + TOK_BUFS - 1 < n_fill)
            def _():
                tok_copy(i + TOK_BUFS - 1).start()

            @pl.when(i >= 2)
            def _():
                c_copy(i).wait()

            cbuf[lax.rem(i, 2)] = row_softmax(scaled_logits(tokbuf[lax.rem(i, TOK_BUFS)], v_ref[...], g_ref[0]))
            c_copy(i).start()
            return carry

        lax.fori_loop(lo, hi, one, 0)

    state = {}

    def factor():
        for d in mz_sends:
            d.wait_recv()
        tops = [mz_all[q, 0] for q in range(n_seq)]
        top = functools.reduce(jnp.maximum, tops)
        z = functools.reduce(jnp.add, [mz_all[q, 1] * jnp.exp(tops[q] - top) for q in range(n_seq)])
        state["f"] = jnp.transpose(jnp.exp(mz_ref[0] - top) / z)
        loads[0].wait()

    def scale(k):
        for j in range(bc):
            b = k * bc + j
            val = s_buf[b].astype(jnp.float32) * state["f"][:, b:b + 1]
            val = val.astype(jnp.bfloat16)
            for q in range(n_seq):
                sc[k, q % CORES, j, q // CORES] = val[q * slots:(q + 1) * slots]
        state["d2d", k] = send(sc.at[k, oc], dr.at[k], twin)

    def ring_send(tag, k, buf, far, r, l, f, rcv, size, rdev, ldev):
        lo, hi = pl.ds(0, size // 2), pl.ds(size // 2, size // 2)
        state[tag, k, 0] = (send(buf.at[k, far, lo], f.at[k, 0], rdev), send(buf.at[k, far, hi], f.at[k, 1], ldev))
        state[tag, k, 1] = [send(buf.at[k, r, hi], rcv.at[k, 0, hi], rdev), send(buf.at[k, l, lo], rcv.at[k, 1, lo], ldev)]

    def ring_relay(tag, k, buf, r, l, f, relay, rcv, size, rdev, ldev):
        half = size // 2
        lo, hi = pl.ds(0, half), pl.ds(half, half)
        for d in state[tag, k, 0]:
            d.wait_recv()
        relay[k, 0] = (buf[k, r, lo].astype(jnp.float32) + f[k, 0].astype(jnp.float32)).astype(jnp.bfloat16)
        relay[k, 1] = (buf[k, l, hi].astype(jnp.float32) + f[k, 1].astype(jnp.float32)).astype(jnp.bfloat16)
        state[tag, k, 1] += [send(relay.at[k, 0], rcv.at[k, 0, lo], rdev), send(relay.at[k, 1], rcv.at[k, 1, hi], ldev)]

    def ring_sum(tag, k, own, rcv):
        for d in state[tag, k, 1]:
            d.wait_recv()
        return (own.astype(jnp.float32) + rcv[k, 0].astype(jnp.float32) + rcv[k, 1].astype(jnp.float32)).astype(jnp.bfloat16)

    def pair(k):
        state["d2d", k].wait_recv()
        for q in range(RING):
            pb[k, q] = (sc[k, c, :, q].astype(jnp.float32) + dr[k, :, q].astype(jnp.float32)).astype(jnp.bfloat16)
        ring_send("x", k, pb, xo, xr, xl, fx, rx, bc, right, left)

    def rsx2(k):
        ring_relay("x", k, pb, xr, xl, fx, sx, rx, bc, right, left)

    def slot_in(k):
        val = ring_sum("x", k, pb[k, x], rx).reshape(n, -1)
        xs[k, m] = jnp.dot(perm_ref[...], val, preferred_element_type=jnp.float32).astype(jnp.bfloat16)
        state["gy", k] = [send(xs.at[k, m], xs.at[k, m], dev) for dev in (up, down)]

    def gy2(k):
        for d in state["gy", k]:
            d.wait_recv()
        lo, hi = pl.ds(0, n // 2), pl.ds(n // 2, n // 2)
        state["gy2", k] = [send(xs.at[k, ml, lo], xs.at[k, ml, lo], up), send(xs.at[k, mr, hi], xs.at[k, mr, hi], down)]

    def experts(k):
        if k == 0:
            loads[1].wait()
            loads[2].wait()
        for d in state["gy2", k]:
            d.wait_recv()
        n_exp = win.shape[0]
        r = n // n_exp
        for e in range(n_exp):
            rows = xs[k, :, e * r:(e + 1) * r, :].reshape(RING * r, -1)
            h = jnp.dot(rows, win[e], preferred_element_type=jnp.float32)
            h = (0.5 * h * (1.0 + lax.erf(h * np.float32(np.sqrt(0.5))))).astype(jnp.bfloat16)
            o = jnp.dot(h, wout[e], preferred_element_type=jnp.float32).astype(jnp.bfloat16)
            op[k, :, e * r:(e + 1) * r, :] = o.reshape(RING, r, -1)
        ring_send("y", k, op, mo, mr, ml, fy, ry, n, up, down)

    def rsy2(k):
        ring_relay("y", k, op, mr, ml, fy, sy, ry, n, up, down)

    def slot_out(k):
        val = ring_sum("y", k, op[k, m], ry)
        val = jnp.dot(permt_ref[...], val, preferred_element_type=jnp.float32).astype(jnp.bfloat16).reshape(bc, slots, -1)
        ysa[k, x, c, m] = val[:bh]
        ysb[k, m, c, x] = val[bh:]
        a, b = ysa.at[k, x, c, m], ysb.at[k, m, c, x]
        state["g1", k] = [send(a, a, up), send(a, a, down), send(b, b, right), send(b, b, left)]

    def ag2(k):
        for d in state["g1", k]:
            d.wait_recv()
        lo, hi = pl.ds(0, bq), pl.ds(bq, bq)
        todo = [(ysa.at[k, x, c, ml, lo], up), (ysa.at[k, x, c, mr, hi], down), (ysb.at[k, m, c, xl, lo], right), (ysb.at[k, m, c, xr, hi], left)]
        state["g2", k] = [send(r, r, dev) for r, dev in todo]

    def ag3(k):
        for d in state["g2", k]:
            d.wait_recv()
        a, b = ysa.at[k, x, c], ysb.at[k, m, c]
        state["g3", k] = [send(a, a, right), send(a, a, left), send(b, b, up), send(b, b, down)]
        state["t", k] = [send(a, a, twin), send(b, b, twin)]

    def ag4(k):
        for d in state["g3", k]:
            d.wait_recv()
        lo, hi = pl.ds(0, RING // 2), pl.ds(RING // 2, RING // 2)
        todo = [(ysa.at[k, xl, c, lo], right), (ysa.at[k, xr, c, hi], left), (ysb.at[k, ml, c, lo], up), (ysb.at[k, mr, c, hi], down)]
        state["g4", k] = [send(r, r, dev) for r, dev in todo]
        state["t", k] += [send(r, r, twin) for r in (ysa.at[k, xl, c], ysa.at[k, xr, c], ysb.at[k, ml, c], ysb.at[k, mr, c])]

    def ag5(k):
        for d in state["g4", k]:
            d.wait_recv()
        state["t", k] += [send(r, r, twin) for r in (ysa.at[k, xo, c], ysb.at[k, mo, c])]

    outs = []

    def finish(k):
        for d in state["t", k]:
            d.wait_recv()
        for i, (a, b) in enumerate(((ysa, ysa_hbm), (ysb, ysb_hbm))):
            d = pltpu.make_async_copy(a.at[k], b.at[k], out_sem.at[2 * k + i])
            d.start()
            outs.append(d)

    stages = {f.__name__: f for f in (scale, pair, rsx2, slot_in, gy2, experts, rsy2, slot_out, ag2, ag3, ag4, ag5, finish)}
    for name, arg in plan:
        if name == "fill":
            fill(arg)
        elif name == "factor":
            factor()
        else:
            stages[name](arg)
    fill(n_fill)
    for d in outs:
        d.wait()
    for d in copies:
        d.wait_send()
    c_copy(jnp.int32(0)).wait()
    c_copy(jnp.int32(1)).wait()


STAGES = ("scale", "pair", "rsx2", "slot_in", "gy2", "experts", "rsy2", "slot_out", "ag2", "ag3", "ag4", "ag5", "finish")


def make_plan(chunks, n_fill):
    ticks = chunks + len(STAGES) - 1
    plan = [("fill", max(1, n_fill // 12)), ("factor", 0)]
    per = -(-(n_fill - n_fill // 12) // max(1, ticks - 4))
    for t in range(ticks):
        for st in reversed(range(len(STAGES))):
            if 0 <= t - st < chunks:
                plan.append((STAGES[st], t - st))
        plan.append(("fill", per))
    return tuple(plan)


def combine_kernel(pos_ref, len_ref, c0_ref, c1_ref, ysa_ref, ysb_ref, y_ref):
    r, k, h = pl.program_id(0), pl.program_id(1), pl.program_id(2)
    bh, toks = y_ref.shape[0], y_ref.shape[1]
    group = pl.num_programs(1) * 2 * bh
    base = lax.rem(pos_ref[0] + r, RING) * group + (k * 2 + h) * bh
    first = pos_ref[1] * toks

    def emit(c_ref, table):
        for j in range(bh):
            mixed = jnp.dot(c_ref[j], table(j), preferred_element_type=jnp.float32)
            valid = first + lax.broadcasted_iota(jnp.int32, mixed.shape, 0) < len_ref[base + j]
            y_ref[j] = jnp.where(valid, mixed, 0.0).astype(y_ref.dtype)

    def table_a(j):
        return ysa_ref[0, :, :, 0, j].reshape(-1, y_ref.shape[2])

    def table_b(j):
        return jnp.concatenate([ysb_ref[0, 0, q % CORES, q // CORES, j] for q in range(CORES * RING)], axis=0)

    for first_group, c_ref in ((True, c0_ref), (False, c1_ref)):
        for half, table in ((0, table_a), (1, table_b)):
            @pl.when(((r == 0) == first_group) & (h == half))
            def _(c_ref=c_ref, table=table):
                emit(c_ref, table)


def solution(mesh):
    n_seq, n_model = mesh.shape["seq"], mesh.shape["model"]
    assert n_model == RING and n_seq == RING * CORES

    def local_layer(tokens, lengths, slot_params, logit_scale, w_in, w_out):
        batch, toks, dim = tokens.shape
        n_slots = slot_params.shape[1]
        slots = n_slots // n_seq
        n_exp = w_in.shape[0]
        group = batch // n_model
        bc = group // CHUNKS
        bh, n = bc // 2, bc * slots
        n_fill = batch - group
        bf16, f32 = jnp.bfloat16, jnp.float32
        unit = unit_vectors(slot_params, 0)
        g = logit_scale.reshape(1)
        pos = jnp.stack([lax.axis_index("model"), lax.axis_index("seq")]).astype(jnp.int32)

        part, mz, c0 = pl.pallas_call(
            dispatch_kernel,
            grid_spec=pltpu.PrefetchScalarGridSpec(
                num_scalar_prefetch=3,
                grid=(group,),
                in_specs=[
                    pl.BlockSpec((1, toks, dim), lambda i, pos, lens, g: (pos[0] * group + i, 0, 0)),
                    pl.BlockSpec((dim, n_slots), lambda i, pos, lens, g: (0, 0)),
                ],
                out_specs=[
                    pl.BlockSpec((1, n_slots, dim), lambda i, pos, lens, g: (i, 0, 0)),
                    pl.BlockSpec((2, group, n_slots), lambda i, pos, lens, g: (0, 0, 0)),
                    pl.BlockSpec((1, toks, n_slots), lambda i, pos, lens, g: (i, 0, 0)),
                ],
            ),
            out_shape=[
                jax.ShapeDtypeStruct((group, n_slots, dim), bf16),
                jax.ShapeDtypeStruct((2, group, n_slots), f32),
                jax.ShapeDtypeStruct((group, toks, n_slots), bf16),
            ],
            compiler_params=pltpu.CompilerParams(dimension_semantics=("arbitrary",)),
            name="dispatch",
        )(pos, lengths, g, tokens, unit)

        order = np.arange(n).reshape(bc, n_exp, slots // n_exp).transpose(1, 0, 2).reshape(-1)
        perm = np.zeros((n, n), np.float32)
        perm[np.arange(n), order] = 1.0
        dims = (CHUNKS, bc, n_seq, group, n_fill, slots)
        vmem, hbm = pl.BlockSpec(memory_space=pltpu.VMEM), pl.BlockSpec(memory_space=pl.ANY)
        n_sem = n_seq + 48 * CHUNKS
        ysa, ysb, c1 = pl.pallas_call(
            functools.partial(exchange_kernel, dims, make_plan(CHUNKS, n_fill)),
            in_specs=[hbm, pl.BlockSpec(memory_space=pltpu.SMEM), vmem, hbm, vmem, hbm, hbm, vmem, vmem],
            out_specs=[hbm, hbm, hbm],
            out_shape=[
                jax.ShapeDtypeStruct((CHUNKS, RING, CORES, RING, bh, slots, dim), bf16),
                jax.ShapeDtypeStruct((CHUNKS, RING, CORES, RING, bh, slots, dim), bf16),
                jax.ShapeDtypeStruct((n_fill, toks, n_slots), bf16),
            ],
            scratch_shapes=[
                pltpu.VMEM((TOK_BUFS, toks, dim), bf16),
                pltpu.VMEM((2, toks, n_slots), bf16),
                pltpu.VMEM((group, n_slots, dim), bf16),
                pltpu.VMEM((n_seq, 2, group, n_slots), f32),
                pltpu.VMEM(w_in.shape, bf16),
                pltpu.VMEM(w_out.shape, bf16),
                pltpu.VMEM((CHUNKS, CORES, bc, RING, slots, dim), bf16),
                pltpu.VMEM((CHUNKS, bc, RING, slots, dim), bf16),
                pltpu.VMEM((CHUNKS, RING, bc, slots, dim), bf16),
                pltpu.VMEM((CHUNKS, 2, bh, slots, dim), bf16),
                pltpu.VMEM((CHUNKS, 2, bh, slots, dim), bf16),
                pltpu.VMEM((CHUNKS, 2, bc, slots, dim), bf16),
                pltpu.VMEM((CHUNKS, RING, n, dim), bf16),
                pltpu.VMEM((CHUNKS, RING, n, dim), bf16),
                pltpu.VMEM((CHUNKS, 2, n // 2, dim), bf16),
                pltpu.VMEM((CHUNKS, 2, n // 2, dim), bf16),
                pltpu.VMEM((CHUNKS, 2, n, dim), bf16),
                pltpu.VMEM((CHUNKS, RING, CORES, RING, bh, slots, dim), bf16),
                pltpu.VMEM((CHUNKS, RING, CORES, RING, bh, slots, dim), bf16),
                pltpu.SemaphoreType.DMA((TOK_BUFS,)),
                pltpu.SemaphoreType.DMA((2,)),
                pltpu.SemaphoreType.DMA((3,)),
                pltpu.SemaphoreType.DMA((2 * CHUNKS,)),
                pltpu.SemaphoreType.DMA((n_sem,)),
                pltpu.SemaphoreType.DMA((n_sem,)),
            ],
            compiler_params=pltpu.CompilerParams(collective_id=0, has_side_effects=True, vmem_limit_bytes=VMEM_LIMIT),
            name="exchange",
        )(tokens, g, unit, part, mz, w_in, w_out, jnp.asarray(perm, bf16), jnp.asarray(perm.T, bf16))

        per = group // bh
        y_grid = (RING, CHUNKS, 2)
        return pl.pallas_call(
            combine_kernel,
            grid_spec=pltpu.PrefetchScalarGridSpec(
                num_scalar_prefetch=2,
                grid=y_grid,
                in_specs=[
                    pl.BlockSpec((bh, toks, n_slots), lambda r, k, h, pos, lens: (jnp.where(r == 0, k * 2 + h, per - 1), 0, 0)),
                    pl.BlockSpec((bh, toks, n_slots), lambda r, k, h, pos, lens: (jnp.where(r == 0, 0, (r - 1) * per + k * 2 + h), 0, 0)),
                    pl.BlockSpec((1, RING, CORES, 1, bh, slots, dim), lambda r, k, h, pos, lens: (k, 0, 0, lax.rem(pos[0] + r, RING), 0, 0, 0)),
                    pl.BlockSpec((1, 1, CORES, RING, bh, slots, dim), lambda r, k, h, pos, lens: (k, lax.rem(pos[0] + r, RING), 0, 0, 0, 0, 0)),
                ],
                out_specs=pl.BlockSpec((bh, toks, dim), lambda r, k, h, pos, lens: (lax.rem(pos[0] + r, RING) * per + k * 2 + h, 0, 0)),
            ),
            out_shape=jax.ShapeDtypeStruct(tokens.shape, tokens.dtype),
            compiler_params=pltpu.CompilerParams(dimension_semantics=("arbitrary",) * 3, vmem_limit_bytes=VMEM_LIMIT),
            name="combine",
        )(pos, lengths, c0, c1, ysa, ysb)

    return jax.shard_map(local_layer, mesh=mesh, in_specs=(P("data", "seq", None), P("data"), P(), P(), P("seq", None, "model"), P("seq", "model", None)), out_specs=P("data", "seq", None), check_vma=False)
```

time: 364 us -> 161 us (0.44)
  Pallas kernels: 0 us -> 155 us
  waiting for transfers between devices: 119 us -> 0 us
  matrix products: 95 us -> 0 us
  blocking collectives: 83.1 us -> 0 us
  other arithmetic: 49.3 us -> 3.34 us
  between operations: 13.9 us -> 0.66 us
  local copies, waits for them, and re-layouts: 4.03 us -> 0 us
    pallas_call x0 -> x3, Pallas kernels: none -> 155 us  [the longest x1 101 us: local_layer(): pl.pallas_call(functools.partial(exchange_kernel, dims, make_plan(CHUNKS,...]
    dot_general x4 -> x0, matrix products: 95 us -> none  [the longest x1 30.6 us: local_layer(): jnp.einsum('bmn,bnd->bmd', mix_weights, all_slots, preferred_element_type...]
    reduce_scatter x1 -> x0, waiting for transfers between devices: 72.6 us -> none  [local_layer(): lax.psum_scatter(part_sum.astype(jnp.bfloat16), 'seq', scatter_dimension=...]
    psum x1 -> x0, blocking collectives: 59.1 us -> none  [local_layer(): lax.psum(out_part, 'model').astype(jnp.bfloat16)]
    all_gather x1 -> x0, waiting for transfers between devices: 45.8 us -> none  [local_layer(): all_slots = lax.all_gather(slot_out, 'seq', axis=1, tiled=True)]
    pmax x1 -> x0, blocking collectives: 24 us -> none  [local_layer(): col_max = lax.pmax(jnp.max(masked, axis=1, keepdims=True), 'seq')]
    sub x1 -> x0, other arithmetic: 22 us -> none  [local_layer(): mix_weights = jax.nn.softmax(logits, axis=-1).astype(jnp.bfloat16)]
    reduce_sum x2 -> x1, other arithmetic: 18.1 us -> 1.04 us  [unit_vectors(): jnp.sum(v32 * v32, axis=axis, keepdims=True) + NORM_EPS]
  transfers between devices with their start and end apart: 3 -> 0, of which waited for: 3 -> 0; matrix products, arithmetic and copies ran while one was open for 14% -> 0% of each run, Pallas kernels for 0% -> 0%
where the time goes in v1:
time: 161 us; the launch traced here: 159 us
  Pallas kernels  155 us (96%)
  other arithmetic  3.34 us (2%)
    pallas_call x1, Pallas kernels, local_layer(): pl.pallas_call(functools.partial(exchange_kernel, dims, make_plan(CHUNKS,...  101 us
    pallas_call x1, Pallas kernels, local_layer(): pl.pallas_call(combine_kernel, grid_spec=pltpu.PrefetchScalarGridSpec(num...  34.5 us
    pallas_call x1, Pallas kernels, local_layer(): pl.pallas_call(dispatch_kernel, grid_spec=pltpu.PrefetchScalarGridSpec(nu...  19.9 us

profile of v1, /device:TPU:97, one launch (start us, length us, event | category | flops | bytes accessed | tf_op | source)
XLA Modules:
  0.0 159.3 jit_solution(11995452457029436524)
XLA Ops:
  0.7 0.6 pad_add_fusion.pos_ref
  1.3 1.0 fusion
  2.4 1.6 %fusion.1.v_ref = bf16[768,128]{1,0:T(8,128)(2,1)} fusion(bf16[768,128]{1,0:T(8,128)(2,1)} %param.10, f32[128]{0:T(128)S(1)} %add_rsqrt_fusion), kind=kLoop, calls=%fused_computation.3 | loop fusion | flops 294912 | bytes 393728 | tf_op jit(solution)/shard_map/convert_element_type | solution.py:23
  4.0 19.9 %dispatch.1 = (bf16[16,128,768]{2,1,0:T(8,128)(2,1)}, f32[2,16,128]{2,1,0:T(8,128)}, bf16[16,512,128]{2,1,0:T(8,128)(2,1)}) custom-call(s32[2]{0:T(128)} %pad_add_fusion.pos_ref, s32[64]{0:T(128)} %len_ref.3, f32[1]{0:T(128)} %bitcast.3.g_ref, bf16[64,512,768]{2,1,0:T(8,128)(2,1)} %tok_hbm.1, bf16[768,128]{1,0:T(8,128)(2,1)} %fusion.1.v_ref), custom_call_target="tpu_custom_call" | custom-call | tf_op jit(solution)/shard_map/dispatch/pallas_call | solution.py:330
  23.9 100.8 %exchange.1 = (bf16[2,4,2,4,4,16,768]{6,5,4,3,2,1,0:T(8,128)(2,1)}, bf16[2,4,2,4,4,16,768]{6,5,4,3,2,1,0:T(8,128)(2,1)}, bf16[48,512,128]{2,1,0:T(8,128)(2,1)}) custom-call(bf16[64,512,768]{2,1,0:T(8,128)(2,1)} %tok_hbm.1, f32[1]{0:T(128)} %bitcast.4.g_ref, bf16[768,128]{1,0:T(8,128)(2,1)} %fusion.1.v_ref, bf16[16,128,768]{2,1,0:T(8,128)(2,1)} %get-tuple-element.12.s_hbm, ...), custom_call_target="tpu_custom_call" | custom-call | tf_op jit(solution)/shard_map/exchange/pallas_call | solution.py:360
  124.8 34.5 %combine.1 = bf16[64,512,768]{2,1,0:T(8,128)(2,1)} custom-call(s32[2]{0:T(128)} %pad_add_fusion.pos_ref, s32[64]{0:T(128)} %len_ref.3, bf16[16,512,128]{2,1,0:T(8,128)(2,1)} %get-tuple-element.11.c0_ref, bf16[48,512,128]{2,1,0:T(8,128)(2,1)} %get-tuple-element.14.c1_ref, bf16[2,4,2,4,4,16,768]{6,5,4,3,2,1,0:T(8,128)(2,1)} %get-tuple-element.15.ysa_ref, ...), custom_call_target="tpu_custom_call" | custom-call | tf_op jit(solution)/shard_map/combine/pallas_call | solution.py:402
  (1 shorter events, 0.0 us)

commit v2 on v1

v2 whole, which is shorter than its diff:
```python
import functools

import jax
import jax.numpy as jnp
import numpy as np
from jax import lax
from jax.experimental import pallas as pl
from jax.experimental.pallas import tpu as pltpu
from jax.sharding import PartitionSpec as P

NORM_EPS = 1e-6
NEG = -1e30
MESH = pl.DeviceIdType.MESH
CORES = 2
RING = 4
CHUNKS = 4
PAIR = 2
TOK_BUFS = 3
OUT_BUFS = 4
PLAN = (
    ("dispatch", 0), ("dispatch", 1), ("scale", 0), ("dispatch", 2), ("scale", 1), ("pair", 0), ("dispatch", 3),
    ("rsx2", 0), ("scale", 2), ("pair", 1), ("fill", 6), ("slot_in", 0), ("rsx2", 1), ("scale", 3), ("pair", 2),
    ("fill", 6), ("slot_in", 1), ("rsx2", 2), ("gy2", 0), ("pair", 3), ("fill", 6), ("slot_in", 2), ("rsx2", 3),
    ("experts", 0), ("gy2", 1), ("fill", 6), ("rsy2", 0), ("slot_in", 3), ("gy2", 2), ("fill", 6), ("slot_out", 0),
    ("experts", 1), ("gy2", 3), ("fill", 6), ("ag2", 0), ("rsy2", 1), ("experts", 2), ("experts", 3), ("ag3", 0),
    ("slot_out", 1), ("rsy2", 2), ("fill", 6), ("rsy2", 3), ("fill", 6), ("ag4", 0), ("ag2", 1), ("slot_out", 2),
    ("slot_out", 3), ("ag5", 0), ("ag3", 1), ("ag2", 2), ("finish", 0), ("ag2", 3), ("ag4", 1), ("ag3", 2),
    ("ag3", 3), ("ag5", 1), ("finish", 1), ("ag4", 2), ("ag4", 3), ("ag5", 2), ("ag5", 3), ("finish", 2),
    ("finish", 3),
)
VMEM_LIMIT = 60 * 1024 * 1024


def unit_vectors(values, axis):
    v32 = values.astype(jnp.float32)
    return (v32 * lax.rsqrt(jnp.sum(v32 * v32, axis=axis, keepdims=True) + NORM_EPS)).astype(jnp.bfloat16)


def scaled_logits(x, v, g):
    return g * jnp.dot(unit_vectors(x, 1), v, preferred_element_type=jnp.float32)


def row_softmax(logits):
    e = jnp.exp(logits - jnp.max(logits, axis=1, keepdims=True))
    return (e * (1.0 / jnp.sum(e, axis=1, keepdims=True))).astype(jnp.bfloat16)


def exchange_kernel(dims, plan, tok_hbm, len_ref, g_ref, phi_ref, win_hbm, wout_hbm, perm_ref, permt_ref,
                    ysa_hbm, ysb_hbm, c_hbm,
                    tokbuf, cbuf, unit, s_buf, mz_loc, mz_all, win, wout, sc, dr, pb, fx, sx, rx, xs, op, fy, sy, ry, ysa, ysb,
                    tok_sem, c_sem, load_sem, out_sem, send_sem, recv_sem):
    chunks, bc, n_seq, group, slots = dims
    bh, bq = bc // 2, bc // 4
    n = bc * slots
    batch, toks = tok_hbm.shape[0], tok_hbm.shape[1]
    m, s = lax.axis_index("model"), lax.axis_index("seq")
    c, x = lax.rem(s, CORES), lax.div(s, CORES)
    oc = 1 - c
    xr, xl, xo = lax.rem(x + 1, RING), lax.rem(x + RING - 1, RING), lax.rem(x + 2, RING)
    mr, ml, mo = lax.rem(m + 1, RING), lax.rem(m + RING - 1, RING), lax.rem(m + 2, RING)
    right, left = {"seq": xr * CORES + c}, {"seq": xl * CORES + c}
    up, down = {"model": mr}, {"model": ml}
    twin = {"seq": x * CORES + oc}
    row_peers = [{"seq": lax.rem(s + d, n_seq)} for d in range(1, n_seq)]
    peers = row_peers + [up, down]
    n_pairs = batch // PAIR

    def tok_copy(p):
        slot = lax.rem(p, TOK_BUFS)
        b = lax.rem(m * group + p * PAIR, batch)
        return pltpu.make_async_copy(tok_hbm.at[pl.ds(b, PAIR)], tokbuf.at[slot], tok_sem.at[slot])

    def c_copy(p):
        slot = lax.rem(p, 2)
        return pltpu.make_async_copy(cbuf.at[slot], c_hbm.at[pl.ds(p * PAIR, PAIR)], c_sem.at[slot])

    for p in range(TOK_BUFS - 1):
        tok_copy(jnp.int32(p)).start()
    loads = [pltpu.make_async_copy(a, b, load_sem.at[i]) for i, (a, b) in enumerate(((win_hbm, win), (wout_hbm, wout)))]
    for ld in loads:
        ld.start()

    barrier = pltpu.get_barrier_semaphore()
    for peer in peers:
        pl.semaphore_signal(barrier, inc=1, device_id=peer, device_id_type=MESH)
    unit[...] = unit_vectors(phi_ref[...], 0)
    mz_loc[...] = jnp.zeros_like(mz_loc)

    def next_pair(p):
        tok_copy(p).wait()

        @pl.when(p + TOK_BUFS - 1 < n_pairs)
        def _():
            tok_copy(p + TOK_BUFS - 1).start()

        @pl.when(p >= 2)
        def _():
            c_copy(p).wait()

        return lax.rem(p, TOK_BUFS), lax.rem(p, 2)

    copies = []

    def send(src, dst, dev):
        i = len(copies)
        d = pltpu.make_async_remote_copy(src_ref=src, dst_ref=dst, send_sem=send_sem.at[i], recv_sem=recv_sem.at[i], device_id=dev, device_id_type=MESH)
        d.start()
        copies.append(d)
        return d

    state = {}

    def dispatch(k):
        def one(j, carry):
            p = k * (bc // PAIR) + j
            slot, c_slot = next_pair(p)
            for q in range(PAIR):
                i = p * PAIR + q
                seq = tokbuf[slot, q]
                logits = scaled_logits(seq, unit[...], g_ref[0])
                cbuf[c_slot, q] = row_softmax(logits)
                valid = s * toks + lax.broadcasted_iota(jnp.int32, logits.shape, 0) < len_ref[m * group + i]
                masked = jnp.where(valid, logits, NEG)
                top = jnp.max(masked, axis=0, keepdims=True)
                w = jnp.where(valid, jnp.exp(masked - top), 0.0)
                mz_loc[k, 0, pl.ds(j * PAIR + q, 1), :] = top
                mz_loc[k, 1, pl.ds(j * PAIR + q, 1), :] = jnp.sum(w, axis=0, keepdims=True)
                s_buf[i] = lax.dot_general(w.astype(jnp.bfloat16), seq, (((0,), (0,)), ((), ())), preferred_element_type=jnp.float32)
            c_copy(p).start()
            return carry

        lax.fori_loop(0, bc // PAIR, one, 0)
        if k == 0:
            pl.semaphore_wait(barrier, len(peers))
        state["mz", k] = [send(mz_loc.at[k], mz_all.at[k, s], peer) for peer in row_peers]
        mz_all[k, s] = mz_loc[k]

    filled = [group // PAIR]

    def fill(count):
        lo = filled[0]
        hi = min(lo + count // PAIR, n_pairs)
        filled[0] = hi
        if hi == lo:
            return

        def one(p, carry):
            slot, c_slot = next_pair(p)
            half = toks // 2
            for q in range(PAIR):
                for r in range(0, toks, half):
                    cbuf[c_slot, q, r:r + half] = row_softmax(scaled_logits(tokbuf[slot, q, r:r + half], unit[...], g_ref[0]))
            c_copy(p).start()
            return carry

        lax.fori_loop(lo, hi, one, 0)

    def scale(k):
        for d in state["mz", k]:
            d.wait_recv()
        tops = [mz_all[k, q, 0] for q in range(n_seq)]
        top = functools.reduce(jnp.maximum, tops)
        z = functools.reduce(jnp.add, [mz_all[k, q, 1] * jnp.exp(tops[q] - top) for q in range(n_seq)])
        f = jnp.transpose(jnp.exp(mz_loc[k, 0] - top) / z)
        for j in range(bc):
            val = (s_buf[k * bc + j] * f[:, j:j + 1]).astype(jnp.bfloat16)
            for q in range(n_seq):
                sc[k, q % CORES, j, q // CORES] = val[q * slots:(q + 1) * slots]
        state["d2d", k] = send(sc.at[k, oc], dr.at[k], twin)

    def ring_send(tag, k, buf, far, r, l, f, rcv, size, rdev, ldev):
        lo, hi = pl.ds(0, size // 2), pl.ds(size // 2, size // 2)
        state[tag, k, 0] = (send(buf.at[k, far, lo], f.at[k, 0], rdev), send(buf.at[k, far, hi], f.at[k, 1], ldev))
        state[tag, k, 1] = [send(buf.at[k, r, hi], rcv.at[k, 0, hi], rdev), send(buf.at[k, l, lo], rcv.at[k, 1, lo], ldev)]

    def ring_relay(tag, k, buf, r, l, f, relay, rcv, size, rdev, ldev):
        half = size // 2
        lo, hi = pl.ds(0, half), pl.ds(half, half)
        for d in state[tag, k, 0]:
            d.wait_recv()
        relay[k, 0] = (buf[k, r, lo].astype(jnp.float32) + f[k, 0].astype(jnp.float32)).astype(jnp.bfloat16)
        relay[k, 1] = (buf[k, l, hi].astype(jnp.float32) + f[k, 1].astype(jnp.float32)).astype(jnp.bfloat16)
        state[tag, k, 1] += [send(relay.at[k, 0], rcv.at[k, 0, lo], rdev), send(relay.at[k, 1], rcv.at[k, 1, hi], ldev)]

    def ring_sum(tag, k, own, rcv):
        for d in state[tag, k, 1]:
            d.wait_recv()
        return (own.astype(jnp.float32) + rcv[k, 0].astype(jnp.float32) + rcv[k, 1].astype(jnp.float32)).astype(jnp.bfloat16)

    def pair(k):
        state["d2d", k].wait_recv()
        for q in range(RING):
            pb[k, q] = (sc[k, c, :, q].astype(jnp.float32) + dr[k, :, q].astype(jnp.float32)).astype(jnp.bfloat16)
        ring_send("x", k, pb, xo, xr, xl, fx, rx, bc, right, left)

    def rsx2(k):
        ring_relay("x", k, pb, xr, xl, fx, sx, rx, bc, right, left)

    def slot_in(k):
        val = ring_sum("x", k, pb[k, x], rx).reshape(n, -1)
        xs[k, m] = jnp.dot(perm_ref[...], val, preferred_element_type=jnp.float32).astype(jnp.bfloat16)
        state["gy", k] = [send(xs.at[k, m], xs.at[k, m], dev) for dev in (up, down)]

    def gy2(k):
        for d in state["gy", k]:
            d.wait_recv()
        lo, hi = pl.ds(0, n // 2), pl.ds(n // 2, n // 2)
        state["gy2", k] = [send(xs.at[k, ml, lo], xs.at[k, ml, lo], up), send(xs.at[k, mr, hi], xs.at[k, mr, hi], down)]

    def experts(k):
        if k == 0:
            for ld in loads:
                ld.wait()
        for d in state["gy2", k]:
            d.wait_recv()
        n_exp = win.shape[0]
        r = n // n_exp
        for e in range(n_exp):
            rows = xs[k, :, e * r:(e + 1) * r, :].reshape(RING * r, -1)
            h = jnp.dot(rows, win[e], preferred_element_type=jnp.float32)
            h = (0.5 * h * (1.0 + lax.erf(h * np.float32(np.sqrt(0.5))))).astype(jnp.bfloat16)
            o = jnp.dot(h, wout[e], preferred_element_type=jnp.float32).astype(jnp.bfloat16)
            op[k, :, e * r:(e + 1) * r, :] = o.reshape(RING, r, -1)
        ring_send("y", k, op, mo, mr, ml, fy, ry, n, up, down)

    def rsy2(k):
        ring_relay("y", k, op, mr, ml, fy, sy, ry, n, up, down)

    def slot_out(k):
        val = ring_sum("y", k, op[k, m], ry)
        val = jnp.dot(permt_ref[...], val, preferred_element_type=jnp.float32).astype(jnp.bfloat16).reshape(bc, slots, -1)
        ysa[k, x, c, m] = val[:bh]
        ysb[k, m, c, x] = val[bh:]
        a, b = ysa.at[k, x, c, m], ysb.at[k, m, c, x]
        state["g1", k] = [send(a, a, up), send(a, a, down), send(b, b, right), send(b, b, left)]

    def ag2(k):
        for d in state["g1", k]:
            d.wait_recv()
        lo, hi = pl.ds(0, bq), pl.ds(bq, bq)
        todo = [(ysa.at[k, x, c, ml, lo], up), (ysa.at[k, x, c, mr, hi], down), (ysb.at[k, m, c, xl, lo], right), (ysb.at[k, m, c, xr, hi], left)]
        state["g2", k] = [send(r, r, dev) for r, dev in todo]

    def ag3(k):
        for d in state["g2", k]:
            d.wait_recv()
        a, b = ysa.at[k, x, c], ysb.at[k, m, c]
        state["g3", k] = [send(a, a, right), send(a, a, left), send(b, b, up), send(b, b, down)]
        state["t", k] = [send(a, a, twin), send(b, b, twin)]

    def ag4(k):
        for d in state["g3", k]:
            d.wait_recv()
        lo, hi = pl.ds(0, RING // 2), pl.ds(RING // 2, RING // 2)
        todo = [(ysa.at[k, xl, c, lo], right), (ysa.at[k, xr, c, hi], left), (ysb.at[k, ml, c, lo], up), (ysb.at[k, mr, c, hi], down)]
        state["g4", k] = [send(r, r, dev) for r, dev in todo]
        state["t", k] += [send(r, r, twin) for r in (ysa.at[k, xl, c], ysa.at[k, xr, c], ysb.at[k, ml, c], ysb.at[k, mr, c])]

    def ag5(k):
        for d in state["g4", k]:
            d.wait_recv()
        state["t", k] += [send(r, r, twin) for r in (ysa.at[k, xo, c], ysb.at[k, mo, c])]

    outs = []

    def finish(k):
        for d in state["t", k]:
            d.wait_recv()
        for i, (a, b) in enumerate(((ysa, ysa_hbm), (ysb, ysb_hbm))):
            d = pltpu.make_async_copy(a.at[k], b.at[k], out_sem.at[2 * k + i])
            d.start()
            outs.append(d)

    stages = {f.__name__: f for f in (dispatch, fill, scale, pair, rsx2, slot_in, gy2, experts, rsy2, slot_out, ag2, ag3, ag4, ag5, finish)}
    for name, arg in plan:
        stages[name](arg)
    fill(batch)
    for d in outs:
        d.wait()
    for d in copies:
        d.wait_send()
    for p in range(2):
        c_copy(jnp.int32(p)).wait()


def combine_kernel(dims, c_hbm, len_ref, ysa_hbm, ysb_hbm, y_hbm, cb, ta, tb, yb, in_sem, out_sem):
    chunks, bc, n_seq, group, slots = dims
    bh = bc // 2
    toks, dim = y_hbm.shape[1], y_hbm.shape[2]
    steps = c_hbm.shape[0] // bc
    m, s = lax.axis_index("model"), lax.axis_index("seq")

    def place(i):
        return lax.rem(m + lax.div(i, chunks), RING), lax.rem(i, chunks)

    def reads(i):
        g, k = place(i)
        return [
            pltpu.make_async_copy(c_hbm.at[pl.ds(i * bc, bc)], cb.at[i], in_sem.at[i, 0]),
            pltpu.make_async_copy(ysa_hbm.at[k, :, :, g], ta.at[i], in_sem.at[i, 1]),
            pltpu.make_async_copy(ysb_hbm.at[k, g], tb.at[i], in_sem.at[i, 2]),
        ]

    def write(i):
        g, k = place(i)
        slot = lax.rem(i, OUT_BUFS)
        return pltpu.make_async_copy(yb.at[slot], y_hbm.at[pl.ds(g * group + k * bc, bc)], out_sem.at[slot])

    def start(i, carry):
        for d in reads(i):
            d.start()
        return carry

    lax.fori_loop(0, steps, start, 0)

    def one(i, carry):
        g, k = place(i)
        slot = lax.rem(i, OUT_BUFS)
        for d in reads(i):
            d.wait()

        @pl.when(i >= OUT_BUFS)
        def _():
            write(i).wait()

        for j in range(bc):
            if j < bh:
                table = ta[i, :, :, j].reshape(n_seq * slots, dim)
            else:
                table = jnp.concatenate([tb[i, q % CORES, q // CORES, j - bh] for q in range(n_seq)], axis=0)
            mixed = jnp.dot(cb[i, j], table, preferred_element_type=jnp.float32)
            valid = s * toks + lax.broadcasted_iota(jnp.int32, mixed.shape, 0) < len_ref[g * group + k * bc + j]
            yb[slot, j] = jnp.where(valid, mixed, 0.0).astype(yb.dtype)
        write(i).start()
        return carry

    lax.fori_loop(0, steps, one, 0)
    for i in range(steps - OUT_BUFS, steps):
        write(jnp.int32(i)).wait()


def solution(mesh):
    n_seq, n_model = mesh.shape["seq"], mesh.shape["model"]
    assert n_model == RING and n_seq == RING * CORES

    def local_layer(tokens, lengths, slot_params, logit_scale, w_in, w_out):
        batch, toks, dim = tokens.shape
        n_slots = slot_params.shape[1]
        slots = n_slots // n_seq
        n_exp = w_in.shape[0]
        group = batch // n_model
        bc = group // CHUNKS
        bh, n = bc // 2, bc * slots
        bf16, f32 = jnp.bfloat16, jnp.float32
        g = logit_scale.reshape(1)

        order = np.arange(n).reshape(bc, n_exp, slots // n_exp).transpose(1, 0, 2).reshape(-1)
        perm = np.zeros((n, n), np.float32)
        perm[np.arange(n), order] = 1.0
        dims = (CHUNKS, bc, n_seq, group, slots)
        rows = -(-bc // 8) * 8
        smem = pl.BlockSpec(memory_space=pltpu.SMEM)
        vmem, hbm = pl.BlockSpec(memory_space=pltpu.VMEM), pl.BlockSpec(memory_space=pl.ANY)
        n_sem = (n_seq + 48) * CHUNKS
        ysa, ysb, mix = pl.pallas_call(
            functools.partial(exchange_kernel, dims, PLAN),
            in_specs=[hbm, smem, smem, vmem, hbm, hbm, vmem, vmem],
            out_specs=[hbm, hbm, hbm],
            out_shape=[
                jax.ShapeDtypeStruct((CHUNKS, RING, CORES, RING, bh, slots, dim), bf16),
                jax.ShapeDtypeStruct((CHUNKS, RING, CORES, RING, bh, slots, dim), bf16),
                jax.ShapeDtypeStruct((batch, toks, n_slots), bf16),
            ],
            scratch_shapes=[
                pltpu.VMEM((TOK_BUFS, PAIR, toks, dim), bf16),
                pltpu.VMEM((2, PAIR, toks, n_slots), bf16),
                pltpu.VMEM((dim, n_slots), bf16),
                pltpu.VMEM((group, n_slots, dim), f32),
                pltpu.VMEM((CHUNKS, 2, rows, n_slots), f32),
                pltpu.VMEM((CHUNKS, n_seq, 2, rows, n_slots), f32),
                pltpu.VMEM(w_in.shape, bf16),
                pltpu.VMEM(w_out.shape, bf16),
                pltpu.VMEM((CHUNKS, CORES, bc, RING, slots, dim), bf16),
                pltpu.VMEM((CHUNKS, bc, RING, slots, dim), bf16),
                pltpu.VMEM((CHUNKS, RING, bc, slots, dim), bf16),
                pltpu.VMEM((CHUNKS, 2, bh, slots, dim), bf16),
                pltpu.VMEM((CHUNKS, 2, bh, slots, dim), bf16),
                pltpu.VMEM((CHUNKS, 2, bc, slots, dim), bf16),
                pltpu.VMEM((CHUNKS, RING, n, dim), bf16),
                pltpu.VMEM((CHUNKS, RING, n, dim), bf16),
                pltpu.VMEM((CHUNKS, 2, n // 2, dim), bf16),
                pltpu.VMEM((CHUNKS, 2, n // 2, dim), bf16),
                pltpu.VMEM((CHUNKS, 2, n, dim), bf16),
                pltpu.VMEM((CHUNKS, RING, CORES, RING, bh, slots, dim), bf16),
                pltpu.VMEM((CHUNKS, RING, CORES, RING, bh, slots, dim), bf16),
                pltpu.SemaphoreType.DMA((TOK_BUFS,)),
                pltpu.SemaphoreType.DMA((2,)),
                pltpu.SemaphoreType.DMA((2,)),
                pltpu.SemaphoreType.DMA((2 * CHUNKS,)),
                pltpu.SemaphoreType.DMA((n_sem,)),
                pltpu.SemaphoreType.DMA((n_sem,)),
            ],
            compiler_params=pltpu.CompilerParams(collective_id=0, has_side_effects=True, vmem_limit_bytes=VMEM_LIMIT),
            name="exchange",
        )(tokens, lengths, g, slot_params, w_in, w_out, jnp.asarray(perm, bf16), jnp.asarray(perm.T, bf16))

        steps = batch // bc
        return pl.pallas_call(
            functools.partial(combine_kernel, dims),
            in_specs=[hbm, smem, hbm, hbm],
            out_specs=hbm,
            out_shape=jax.ShapeDtypeStruct(tokens.shape, tokens.dtype),
            scratch_shapes=[
                pltpu.VMEM((steps, bc, toks, n_slots), bf16),
                pltpu.VMEM((steps, RING, CORES, bh, slots, dim), bf16),
                pltpu.VMEM((steps, CORES, RING, bh, slots, dim), bf16),
                pltpu.VMEM((OUT_BUFS, bc, toks, dim), bf16),
                pltpu.SemaphoreType.DMA((steps, 3)),
                pltpu.SemaphoreType.DMA((OUT_BUFS,)),
            ],
            compiler_params=pltpu.CompilerParams(vmem_limit_bytes=VMEM_LIMIT),
            name="combine",
        )(mix, lengths, ysa, ysb)

    return jax.shard_map(local_layer, mesh=mesh, in_specs=(P("data", "seq", None), P("data"), P(), P(), P("seq", None, "model"), P("seq", "model", None)), out_specs=P("data", "seq", None), check_vma=False)
```

time: 161 us -> 129 us (0.80); the launches traced: 159 us -> 129 us
  Pallas kernels: 155 us -> 128 us
  other arithmetic: 3.34 us -> 0 us
    pallas_call x3 -> x2, Pallas kernels: 155 us -> 128 us  [the longest x1 105 us: local_layer(): pl.pallas_call(functools.partial(exchange_kernel, dims, PLAN), in_specs=[...]
    convert_element_type x1 -> x0, other arithmetic: 1.64 us -> none  [unit_vectors(): (v32 * lax.rsqrt(jnp.sum(v32 * v32, axis=axis, keepdims=True) + NORM_EPS)...]
where the time goes in v2:
time: 129 us
  Pallas kernels  128 us (99%)
    pallas_call x1, Pallas kernels, local_layer(): pl.pallas_call(functools.partial(exchange_kernel, dims, PLAN), in_specs=[...  105 us
    pallas_call x1, Pallas kernels, local_layer(): pl.pallas_call(functools.partial(combine_kernel, dims), in_specs=[hbm, sm...  23.3 us

profile of v2, /device:TPU:97, one launch (start us, length us, event | category | flops | bytes accessed | tf_op | source)
XLA Modules:
  0.0 129.2 jit_solution(11285071001280151592)
XLA Ops:
  0.7 105.0 %exchange.1 = (bf16[4,4,2,4,2,16,768]{6,5,4,3,2,1,0:T(8,128)(2,1)}, bf16[4,4,2,4,2,16,768]{6,5,4,3,2,1,0:T(8,128)(2,1)}, bf16[64,512,128]{2,1,0:T(8,128)(2,1)}) custom-call(bf16[64,512,768]{2,1,0:T(8,128)(2,1)} %tok_hbm.1, s32[64]{0:T(128)} %len_ref.3, f32[1]{0:T(128)} %bitcast.1.g_ref, bf16[768,128]{1,0:T(8,128)(2,1)} %phi_ref.1, ...), custom_call_target="tpu_custom_call" | custom-call | tf_op jit(solution)/shard_map/exchange/pallas_call | solution.py:365
  105.7 23.3 %combine.1 = bf16[64,512,768]{2,1,0:T(8,128)(2,1)} custom-call(bf16[64,512,128]{2,1,0:T(8,128)(2,1)} %get-tuple-element.8.c_hbm, s32[64]{0:T(128)} %len_ref.3, bf16[4,4,2,4,2,16,768]{6,5,4,3,2,1,0:T(8,128)(2,1)} %get-tuple-element.9.ysa_hbm, bf16[4,4,2,4,2,16,768]{6,5,4,3,2,1,0:T(8,128)(2,1)} %get-tuple-element.10.ysb_hbm), custom_call_target="tpu_custom_call" | custom-call | tf_op jit(solution)/shard_map/combine/pallas_call | solution.py:408

commit v3 on v2

--- a/solution.py
+++ b/solution.py
@@ -18,17 +18,18 @@
 TOK_BUFS = 3
 OUT_BUFS = 4
 PLAN = (
-    ("dispatch", 0), ("dispatch", 1), ("scale", 0), ("dispatch", 2), ("scale", 1), ("pair", 0), ("dispatch", 3),
-    ("rsx2", 0), ("scale", 2), ("pair", 1), ("fill", 6), ("slot_in", 0), ("rsx2", 1), ("scale", 3), ("pair", 2),
-    ("fill", 6), ("slot_in", 1), ("rsx2", 2), ("gy2", 0), ("pair", 3), ("fill", 6), ("slot_in", 2), ("rsx2", 3),
-    ("experts", 0), ("gy2", 1), ("fill", 6), ("rsy2", 0), ("slot_in", 3), ("gy2", 2), ("fill", 6), ("slot_out", 0),
-    ("experts", 1), ("gy2", 3), ("fill", 6), ("ag2", 0), ("rsy2", 1), ("experts", 2), ("experts", 3), ("ag3", 0),
-    ("slot_out", 1), ("rsy2", 2), ("fill", 6), ("rsy2", 3), ("fill", 6), ("ag4", 0), ("ag2", 1), ("slot_out", 2),
-    ("slot_out", 3), ("ag5", 0), ("ag3", 1), ("ag2", 2), ("finish", 0), ("ag2", 3), ("ag4", 1), ("ag3", 2),
-    ("ag3", 3), ("ag5", 1), ("finish", 1), ("ag4", 2), ("ag4", 3), ("ag5", 2), ("ag5", 3), ("finish", 2),
-    ("finish", 3),
+    ("dispatch", 0), ("dispatch", 1), ("scale", 0), ("dispatch", 2), ("pair", 0), ("scale", 1), ("pair", 1),
+    ("rsx2", 0), ("scale", 2), ("dispatch", 3), ("pair", 2), ("slot_in", 0), ("rsx2", 1), ("scale", 3), ("rsx2", 2),
+    ("gy2", 0), ("pair", 3), ("slot_in", 1), ("slot_in", 2), ("rsx2", 3), ("experts", 0), ("gy2", 2), ("gy2", 1),
+    ("slot_in", 3), ("fill", 6), ("rsy2", 0), ("experts", 2), ("experts", 1), ("rsy2", 2), ("gy2", 3),
+    ("slot_out", 0), ("fill", 6), ("rsy2", 1), ("slot_out", 2), ("experts", 3), ("ag2", 2), ("slot_out", 1),
+    ("rsy2", 3), ("ag3", 2), ("ag2", 0), ("slot_out", 3), ("fill", 6), ("ag2", 1), ("ag4", 2), ("ag2", 3),
+    ("ag3", 1), ("ag3", 0), ("fill", 6), ("ag3", 3), ("ag5", 2), ("fill", 6), ("ag4", 1), ("fill", 6), ("ag4", 0),
+    ("fill", 6), ("ag4", 3), ("fill", 6), ("finish", 2), ("ag5", 1), ("ag5", 0), ("ag5", 3), ("finish", 3),
+    ("finish", 0), ("finish", 1),
 )
-VMEM_LIMIT = 60 * 1024 * 1024
+EXCHANGE_VMEM = 42 * 1024 * 1024
+COMBINE_VMEM = 20 * 1024 * 1024
 
 
 def unit_vectors(values, axis):
@@ -46,9 +47,9 @@
 
 
 def exchange_kernel(dims, plan, tok_hbm, len_ref, g_ref, phi_ref, win_hbm, wout_hbm, perm_ref, permt_ref,
-                    ysa_hbm, ysb_hbm, c_hbm,
-                    tokbuf, cbuf, unit, s_buf, mz_loc, mz_all, win, wout, sc, dr, pb, fx, sx, rx, xs, op, fy, sy, ry, ysa, ysb,
-                    tok_sem, c_sem, load_sem, out_sem, send_sem, recv_sem):
+                    ysa, ysb, mix,
+                    tokbuf, unit, s_buf, mz_loc, mz_all, win, wout, sc, dr, pb, fx, sx, rx, xs, op, fy, sy, ry,
+                    tok_sem, load_sem, send_sem, recv_sem):
     chunks, bc, n_seq, group, slots = dims
     bh, bq = bc // 2, bc // 4
     n = bc * slots
@@ -64,15 +65,12 @@
     row_peers = [{"seq": lax.rem(s + d, n_seq)} for d in range(1, n_seq)]
     peers = row_peers + [up, down]
     n_pairs = batch // PAIR
+    half = toks // 2
 
     def tok_copy(p):
         slot = lax.rem(p, TOK_BUFS)
         b = lax.rem(m * group + p * PAIR, batch)
         return pltpu.make_async_copy(tok_hbm.at[pl.ds(b, PAIR)], tokbuf.at[slot], tok_sem.at[slot])
-
-    def c_copy(p):
-        slot = lax.rem(p, 2)
-        return pltpu.make_async_copy(cbuf.at[slot], c_hbm.at[pl.ds(p * PAIR, PAIR)], c_sem.at[slot])
 
     for p in range(TOK_BUFS - 1):
         tok_copy(jnp.int32(p)).start()
@@ -93,11 +91,7 @@
         def _():
             tok_copy(p + TOK_BUFS - 1).start()
 
-        @pl.when(p >= 2)
-        def _():
-            c_copy(p).wait()
-
-        return lax.rem(p, TOK_BUFS), lax.rem(p, 2)
+        return lax.rem(p, TOK_BUFS)
 
     copies = []
 
@@ -113,20 +107,24 @@
     def dispatch(k):
         def one(j, carry):
             p = k * (bc // PAIR) + j
-            slot, c_slot = next_pair(p)
+            slot = next_pair(p)
             for q in range(PAIR):
                 i = p * PAIR + q
-                seq = tokbuf[slot, q]
-                logits = scaled_logits(seq, unit[...], g_ref[0])
-                cbuf[c_slot, q] = row_softmax(logits)
-                valid = s * toks + lax.broadcasted_iota(jnp.int32, logits.shape, 0) < len_ref[m * group + i]
-                masked = jnp.where(valid, logits, NEG)
-                top = jnp.max(masked, axis=0, keepdims=True)
-                w = jnp.where(valid, jnp.exp(masked - top), 0.0)
+                parts = []
+                for r in range(0, toks, half):
+                    logits = scaled_logits(tokbuf[slot, q, r:r + half], unit[...], g_ref[0])
+                    mix[i, r:r + half] = row_softmax(logits)
+                    valid = s * toks + r + lax.broadcasted_iota(jnp.int32, logits.shape, 0) < len_ref[m * group + i]
+                    parts.append((valid, jnp.where(valid, logits, NEG)))
+                top = functools.reduce(jnp.maximum, [jnp.max(v, axis=0, keepdims=True) for _, v in parts])
+                w = jnp.concatenate([jnp.where(ok, jnp.exp(v - top), 0.0) for ok, v in parts], axis=0)
                 mz_loc[k, 0, pl.ds(j * PAIR + q, 1), :] = top
                 mz_loc[k, 1, pl.ds(j * PAIR + q, 1), :] = jnp.sum(w, axis=0, keepdims=True)
-                s_buf[i] = lax.dot_general(w.astype(jnp.bfloat16), seq, (((0,), (0,)), ((), ())), preferred_element_type=jnp.float32)
-            c_copy(p).start()
+                w = w.astype(jnp.bfloat16)
+                wide = s_buf.shape[2] // 2
+                for d in range(2):
+                    cols = slice(d * wide, (d + 1) * wide)
+                    s_buf[i, :, cols] = lax.dot_general(w, tokbuf[slot, q, :, cols], (((0,), (0,)), ((), ())), preferred_element_type=jnp.float32)
             return carry
 
         lax.fori_loop(0, bc // PAIR, one, 0)
@@ -145,12 +143,10 @@
             return
 
         def one(p, carry):
-            slot, c_slot = next_pair(p)
-            half = toks // 2
+            slot = next_pair(p)
             for q in range(PAIR):
                 for r in range(0, toks, half):
-                    cbuf[c_slot, q, r:r + half] = row_softmax(scaled_logits(tokbuf[slot, q, r:r + half], unit[...], g_ref[0]))
-            c_copy(p).start()
+                    mix[p * PAIR + q, r:r + half] = row_softmax(scaled_logits(tokbuf[slot, q, r:r + half], unit[...], g_ref[0]))
             return carry
 
         lax.fori_loop(lo, hi, one, 0)
@@ -208,9 +204,8 @@
         state["gy2", k] = [send(xs.at[k, ml, lo], xs.at[k, ml, lo], up), send(xs.at[k, mr, hi], xs.at[k, mr, hi], down)]
 
     def experts(k):
-        if k == 0:
-            for ld in loads:
-                ld.wait()
+        while loads:
+            loads.pop().wait()
         for d in state["gy2", k]:
             d.wait_recv()
         n_exp = win.shape[0]
@@ -261,63 +256,36 @@
             d.wait_recv()
         state["t", k] += [send(r, r, twin) for r in (ysa.at[k, xo, c], ysb.at[k, mo, c])]
 
-    outs = []
-
     def finish(k):
         for d in state["t", k]:
             d.wait_recv()
-        for i, (a, b) in enumerate(((ysa, ysa_hbm), (ysb, ysb_hbm))):
-            d = pltpu.make_async_copy(a.at[k], b.at[k], out_sem.at[2 * k + i])
-            d.start()
-            outs.append(d)
 
     stages = {f.__name__: f for f in (dispatch, fill, scale, pair, rsx2, slot_in, gy2, experts, rsy2, slot_out, ag2, ag3, ag4, ag5, finish)}
     for name, arg in plan:
         stages[name](arg)
     fill(batch)
-    for d in outs:
-        d.wait()
     for d in copies:
         d.wait_send()
-    for p in range(2):
-        c_copy(jnp.int32(p)).wait()
-
-
-def combine_kernel(dims, c_hbm, len_ref, ysa_hbm, ysb_hbm, y_hbm, cb, ta, tb, yb, in_sem, out_sem):
+
+
+def combine_kernel(dims, mix, len_ref, ysa, ysb, y_hbm, yb, out_sem):
     chunks, bc, n_seq, group, slots = dims
     bh = bc // 2
     toks, dim = y_hbm.shape[1], y_hbm.shape[2]
-    steps = c_hbm.shape[0] // bc
+    steps = mix.shape[0] // bc
     m, s = lax.axis_index("model"), lax.axis_index("seq")
 
     def place(i):
         return lax.rem(m + lax.div(i, chunks), RING), lax.rem(i, chunks)
-
-    def reads(i):
-        g, k = place(i)
-        return [
-            pltpu.make_async_copy(c_hbm.at[pl.ds(i * bc, bc)], cb.at[i], in_sem.at[i, 0]),
-            pltpu.make_async_copy(ysa_hbm.at[k, :, :, g], ta.at[i], in_sem.at[i, 1]),
-            pltpu.make_async_copy(ysb_hbm.at[k, g], tb.at[i], in_sem.at[i, 2]),
-        ]
 
     def write(i):
         g, k = place(i)
         slot = lax.rem(i, OUT_BUFS)
         return pltpu.make_async_copy(yb.at[slot], y_hbm.at[pl.ds(g * group + k * bc, bc)], out_sem.at[slot])
 
-    def start(i, carry):
-        for d in reads(i):
-            d.start()
-        return carry
-
-    lax.fori_loop(0, steps, start, 0)
-
     def one(i, carry):
         g, k = place(i)
         slot = lax.rem(i, OUT_BUFS)
-        for d in reads(i):
-            d.wait()
 
         @pl.when(i >= OUT_BUFS)
         def _():
@@ -325,10 +293,10 @@
 
         for j in range(bc):
             if j < bh:
-                table = ta[i, :, :, j].reshape(n_seq * slots, dim)
+                table = ysa[k, :, :, g, j].reshape(n_seq * slots, dim)
             else:
-                table = jnp.concatenate([tb[i, q % CORES, q // CORES, j - bh] for q in range(n_seq)], axis=0)
-            mixed = jnp.dot(cb[i, j], table, preferred_element_type=jnp.float32)
+                table = jnp.concatenate([ysb[k, g, q % CORES, q // CORES, j - bh] for q in range(n_seq)], axis=0)
+            mixed = jnp.dot(mix[i * bc + j], table, preferred_element_type=jnp.float32)
             valid = s * toks + lax.broadcasted_iota(jnp.int32, mixed.shape, 0) < len_ref[g * group + k * bc + j]
             yb[slot, j] = jnp.where(valid, mixed, 0.0).astype(yb.dtype)
         write(i).start()
@@ -365,15 +333,14 @@
         ysa, ysb, mix = pl.pallas_call(
             functools.partial(exchange_kernel, dims, PLAN),
             in_specs=[hbm, smem, smem, vmem, hbm, hbm, vmem, vmem],
-            out_specs=[hbm, hbm, hbm],
+            out_specs=[vmem, vmem, vmem],
             out_shape=[
-                jax.ShapeDtypeStruct((CHUNKS, RING, CORES, RING, bh, slots, dim), bf16),
-                jax.ShapeDtypeStruct((CHUNKS, RING, CORES, RING, bh, slots, dim), bf16),
-                jax.ShapeDtypeStruct((batch, toks, n_slots), bf16),
+                pltpu.VMEM((CHUNKS, RING, CORES, RING, bh, slots, dim), bf16),
+                pltpu.VMEM((CHUNKS, RING, CORES, RING, bh, slots, dim), bf16),
+                pltpu.VMEM((batch, toks, n_slots), bf16),
             ],
             scratch_shapes=[
                 pltpu.VMEM((TOK_BUFS, PAIR, toks, dim), bf16),
-                pltpu.VMEM((2, PAIR, toks, n_slots), bf16),
                 pltpu.VMEM((dim, n_slots), bf16),
                 pltpu.VMEM((group, n_slots, dim), f32),
                 pltpu.VMEM((CHUNKS, 2, rows, n_slots), f32),
@@ -391,34 +358,26 @@
                 pltpu.VMEM((CHUNKS, 2, n // 2, dim), bf16),
                 pltpu.VMEM((CHUNKS, 2, n // 2, dim), bf16),
                 pltpu.VMEM((CHUNKS, 2, n, dim), bf16),
-                pltpu.VMEM((CHUNKS, RING, CORES, RING, bh, slots, dim), bf16),
-                pltpu.VMEM((CHUNKS, RING, CORES, RING, bh, slots, dim), bf16),
                 pltpu.SemaphoreType.DMA((TOK_BUFS,)),
                 pltpu.SemaphoreType.DMA((2,)),
-                pltpu.SemaphoreType.DMA((2,)),
-                pltpu.SemaphoreType.DMA((2 * CHUNKS,)),
                 pltpu.SemaphoreType.DMA((n_sem,)),
                 pltpu.SemaphoreType.DMA((n_sem,)),
             ],
-            compiler_params=pltpu.CompilerParams(collective_id=0, has_side_effects=True, vmem_limit_bytes=VMEM_LIMIT),
+            compiler_params=pltpu.CompilerParams(collective_id=0, has_side_effects=True, vmem_limit_bytes=EXCHANGE_VMEM),
             name="exchange",
         )(tokens, lengths, g, slot_params, w_in, w_out, jnp.asarray(perm, bf16), jnp.asarray(perm.T, bf16))
 
-        steps = batch // bc
+        mix, ysa, ysb = (pltpu.with_memory_space_constraint(a, pltpu.VMEM) for a in (mix, ysa, ysb))
         return pl.pallas_call(
             functools.partial(combine_kernel, dims),
-            in_specs=[hbm, smem, hbm, hbm],
+            in_specs=[vmem, smem, vmem, vmem],
             out_specs=hbm,
             out_shape=jax.ShapeDtypeStruct(tokens.shape, tokens.dtype),
             scratch_shapes=[
-                pltpu.VMEM((steps, bc, toks, n_slots), bf16),
-                pltpu.VMEM((steps, RING, CORES, bh, slots, dim), bf16),
-                pltpu.VMEM((steps, CORES, RING, bh, slots, dim), bf16),
                 pltpu.VMEM((OUT_BUFS, bc, toks, dim), bf16),
-                pltpu.SemaphoreType.DMA((steps, 3)),
                 pltpu.SemaphoreType.DMA((OUT_BUFS,)),
             ],
-            compiler_params=pltpu.CompilerParams(vmem_limit_bytes=VMEM_LIMIT),
+            compiler_params=pltpu.CompilerParams(vmem_limit_bytes=COMBINE_VMEM),
             name="combine",
         )(mix, lengths, ysa, ysb)
 

time: 129 us -> 119 us (0.922)
  Pallas kernels: 128 us -> 118 us
    pallas_call x1, Pallas kernels: 23.3 us -> 17.8 us  [local_layer(): pl.pallas_call(functools.partial(combine_kernel, dims), in_specs=[vmem, s...]
    pallas_call x1, Pallas kernels: 105 us -> 100 us  [local_layer(): pl.pallas_call(functools.partial(exchange_kernel, dims, PLAN), in_specs=[...]
where the time goes in v3:
time: 119 us
  Pallas kernels  118 us (99%)
    pallas_call x1, Pallas kernels, local_layer(): pl.pallas_call(functools.partial(exchange_kernel, dims, PLAN), in_specs=[...  100 us
    pallas_call x1, Pallas kernels, local_layer(): pl.pallas_call(functools.partial(combine_kernel, dims), in_specs=[vmem, s...  17.8 us

profile of v3, /device:TPU:97, one launch (start us, length us, event | category | flops | bytes accessed | tf_op | source)
XLA Modules:
  0.0 119.1 jit_solution(14243066980528777280)
XLA Ops:
  0.7 0.0 copy-start
  0.7 100.4 %exchange.1 = (bf16[4,4,2,4,2,16,768]{6,5,4,3,2,1,0:T(8,128)(2,1)S(1)}, bf16[4,4,2,4,2,16,768]{6,5,4,3,2,1,0:T(8,128)(2,1)S(1)}, bf16[64,512,128]{2,1,0:T(8,128)(2,1)S(1)}) custom-call(bf16[64,512,768]{2,1,0:T(8,128)(2,1)} %tok_hbm.1, s32[64]{0:T(128)} %len_ref.3, f32[1]{0:T(128)} %bitcast.1.g_ref, bf16[768,128]{1,0:T(8,128)(2,1)} %phi_ref.1, ...), custom_call_target="tpu_custom_call" | custom-call | tf_op jit(solution)/shard_map/exchange/pallas_call | solution.py:333
  101.1 0.0 copy-done
  101.1 17.8 %combine.1 = bf16[64,512,768]{2,1,0:T(8,128)(2,1)} custom-call(bf16[64,512,128]{2,1,0:T(8,128)(2,1)S(1)} %get-tuple-element.8.mix, s32[64]{0:T(128)S(1)} %copy-done, bf16[4,4,2,4,2,16,768]{6,5,4,3,2,1,0:T(8,128)(2,1)S(1)} %get-tuple-element.9.ysa, bf16[4,4,2,4,2,16,768]{6,5,4,3,2,1,0:T(8,128)(2,1)S(1)} %get-tuple-element.10.ysb), custom_call_target="tpu_custom_call" | custom-call | tf_op jit(solution)/shard_map/combine/pallas_call | solution.py:371
Async XLA Ops:
  0.7 100.4 %copy-start = (s32[64]{0:T(128)S(1)}, s32[64]{0:T(128)}, u32[]{:S(2)}) copy-start(s32[64]{0:T(128)} %len_ref.3) | copy-start | bytes 772

commit v4 on v3

--- a/solution.py
+++ b/solution.py
@@ -19,14 +19,14 @@
 OUT_BUFS = 4
 PLAN = (
     ("dispatch", 0), ("dispatch", 1), ("scale", 0), ("dispatch", 2), ("pair", 0), ("scale", 1), ("pair", 1),
-    ("rsx2", 0), ("scale", 2), ("dispatch", 3), ("pair", 2), ("slot_in", 0), ("rsx2", 1), ("scale", 3), ("rsx2", 2),
-    ("gy2", 0), ("pair", 3), ("slot_in", 1), ("slot_in", 2), ("rsx2", 3), ("experts", 0), ("gy2", 2), ("gy2", 1),
-    ("slot_in", 3), ("fill", 6), ("rsy2", 0), ("experts", 2), ("experts", 1), ("rsy2", 2), ("gy2", 3),
-    ("slot_out", 0), ("fill", 6), ("rsy2", 1), ("slot_out", 2), ("experts", 3), ("ag2", 2), ("slot_out", 1),
-    ("rsy2", 3), ("ag3", 2), ("ag2", 0), ("slot_out", 3), ("fill", 6), ("ag2", 1), ("ag4", 2), ("ag2", 3),
-    ("ag3", 1), ("ag3", 0), ("fill", 6), ("ag3", 3), ("ag5", 2), ("fill", 6), ("ag4", 1), ("fill", 6), ("ag4", 0),
-    ("fill", 6), ("ag4", 3), ("fill", 6), ("finish", 2), ("ag5", 1), ("ag5", 0), ("ag5", 3), ("finish", 3),
-    ("finish", 0), ("finish", 1),
+    ("dispatch", 3), ("rsx2", 1), ("rsx2", 0), ("scale", 2), ("pair", 2), ("scale", 3), ("slot_in", 1), ("pair", 3),
+    ("slot_in", 0), ("rsx2", 2), ("rsx2", 3), ("gy2", 1), ("gy2", 0), ("slot_in", 2), ("slot_in", 3),
+    ("experts", 1), ("fill", 6), ("gy2", 2), ("experts", 0), ("gy2", 3), ("rsy2", 1), ("fill", 6), ("rsy2", 0),
+    ("experts", 2), ("experts", 3), ("slot_out", 1), ("fill", 6), ("rsy2", 2), ("rsy2", 3), ("ag2", 1),
+    ("slot_out", 0), ("slot_out", 2), ("slot_out", 3), ("ag3", 1), ("ag2", 2), ("fill", 6), ("ag2", 3), ("ag2", 0),
+    ("ag4", 1), ("ag3", 2), ("ag3", 3), ("ag3", 0), ("fill", 18), ("agt", 1), ("ag5", 1), ("ag4", 3), ("agt", 3),
+    ("ag4", 0), ("agt", 0), ("ag4", 2), ("finish", 1), ("agt", 2), ("fill", 6), ("ag5", 3), ("ag5", 0), ("ag5", 2),
+    ("finish", 3), ("finish", 0), ("finish", 2),
 )
 EXCHANGE_VMEM = 42 * 1024 * 1024
 COMBINE_VMEM = 20 * 1024 * 1024
@@ -192,10 +192,15 @@
     def rsx2(k):
         ring_relay("x", k, pb, xr, xl, fx, sx, rx, bc, right, left)
 
+    def relayed_first(tag, k, todo):
+        state[tag, k] = [send(first, first, dev) for first, _, dev in todo]
+        state[tag + "r", k] = [send(second, second, dev) for _, second, dev in todo]
+
     def slot_in(k):
         val = ring_sum("x", k, pb[k, x], rx).reshape(n, -1)
         xs[k, m] = jnp.dot(perm_ref[...], val, preferred_element_type=jnp.float32).astype(jnp.bfloat16)
-        state["gy", k] = [send(xs.at[k, m], xs.at[k, m], dev) for dev in (up, down)]
+        lo, hi = xs.at[k, m, pl.ds(0, n // 2)], xs.at[k, m, pl.ds(n // 2, n // 2)]
+        relayed_first("gy", k, [(lo, hi, up), (hi, lo, down)])
 
     def gy2(k):
         for d in state["gy", k]:
@@ -206,7 +211,7 @@
     def experts(k):
         while loads:
             loads.pop().wait()
-        for d in state["gy2", k]:
+        for d in state["gyr", k] + state["gy2", k]:
             d.wait_recv()
         n_exp = win.shape[0]
         r = n // n_exp
@@ -226,8 +231,9 @@
         val = jnp.dot(permt_ref[...], val, preferred_element_type=jnp.float32).astype(jnp.bfloat16).reshape(bc, slots, -1)
         ysa[k, x, c, m] = val[:bh]
         ysb[k, m, c, x] = val[bh:]
-        a, b = ysa.at[k, x, c, m], ysb.at[k, m, c, x]
-        state["g1", k] = [send(a, a, up), send(a, a, down), send(b, b, right), send(b, b, left)]
+        lo, hi = pl.ds(0, bq), pl.ds(bq, bq)
+        a_lo, a_hi, b_lo, b_hi = ysa.at[k, x, c, m, lo], ysa.at[k, x, c, m, hi], ysb.at[k, m, c, x, lo], ysb.at[k, m, c, x, hi]
+        relayed_first("g1", k, [(a_lo, a_hi, up), (a_hi, a_lo, down), (b_lo, b_hi, right), (b_hi, b_lo, left)])
 
     def ag2(k):
         for d in state["g1", k]:
@@ -237,10 +243,12 @@
         state["g2", k] = [send(r, r, dev) for r, dev in todo]
 
     def ag3(k):
-        for d in state["g2", k]:
+        for d in state["g1r", k] + state["g2", k]:
             d.wait_recv()
         a, b = ysa.at[k, x, c], ysb.at[k, m, c]
-        state["g3", k] = [send(a, a, right), send(a, a, left), send(b, b, up), send(b, b, down)]
+        lo, hi = pl.ds(0, RING // 2), pl.ds(RING // 2, RING // 2)
+        a_lo, a_hi, b_lo, b_hi = ysa.at[k, x, c, lo], ysa.at[k, x, c, hi], ysb.at[k, m, c, lo], ysb.at[k, m, c, hi]
+        relayed_first("g3", k, [(a_lo, a_hi, right), (a_hi, a_lo, left), (b_lo, b_hi, up), (b_hi, b_lo, down)])
         state["t", k] = [send(a, a, twin), send(b, b, twin)]
 
     def ag4(k):
@@ -249,6 +257,10 @@
         lo, hi = pl.ds(0, RING // 2), pl.ds(RING // 2, RING // 2)
         todo = [(ysa.at[k, xl, c, lo], right), (ysa.at[k, xr, c, hi], left), (ysb.at[k, ml, c, lo], up), (ysb.at[k, mr, c, hi], down)]
         state["g4", k] = [send(r, r, dev) for r, dev in todo]
+
+    def agt(k):
+        for d in state["g3r", k]:
+            d.wait_recv()
         state["t", k] += [send(r, r, twin) for r in (ysa.at[k, xl, c], ysa.at[k, xr, c], ysb.at[k, ml, c], ysb.at[k, mr, c])]
 
     def ag5(k):
@@ -260,7 +272,7 @@
         for d in state["t", k]:
             d.wait_recv()
 
-    stages = {f.__name__: f for f in (dispatch, fill, scale, pair, rsx2, slot_in, gy2, experts, rsy2, slot_out, ag2, ag3, ag4, ag5, finish)}
+    stages = {f.__name__: f for f in (dispatch, fill, scale, pair, rsx2, slot_in, gy2, experts, rsy2, slot_out, ag2, ag3, ag4, agt, ag5, finish)}
     for name, arg in plan:
         stages[name](arg)
     fill(batch)
@@ -278,10 +290,10 @@
     def place(i):
         return lax.rem(m + lax.div(i, chunks), RING), lax.rem(i, chunks)
 
-    def write(i):
+    def write(i, j):
         g, k = place(i)
         slot = lax.rem(i, OUT_BUFS)
-        return pltpu.make_async_copy(yb.at[slot], y_hbm.at[pl.ds(g * group + k * bc, bc)], out_sem.at[slot])
+        return pltpu.make_async_copy(yb.at[slot, j], y_hbm.at[g * group + k * bc + j], out_sem.at[slot, j])
 
     def one(i, carry):
         g, k = place(i)
@@ -289,7 +301,8 @@
 
         @pl.when(i >= OUT_BUFS)
         def _():
-            write(i).wait()
+            for j in range(bc):
+                write(i, j).wait()
 
         for j in range(bc):
             if j < bh:
@@ -299,12 +312,13 @@
             mixed = jnp.dot(mix[i * bc + j], table, preferred_element_type=jnp.float32)
             valid = s * toks + lax.broadcasted_iota(jnp.int32, mixed.shape, 0) < len_ref[g * group + k * bc + j]
             yb[slot, j] = jnp.where(valid, mixed, 0.0).astype(yb.dtype)
-        write(i).start()
+            write(i, j).start()
         return carry
 
     lax.fori_loop(0, steps, one, 0)
     for i in range(steps - OUT_BUFS, steps):
-        write(jnp.int32(i)).wait()
+        for j in range(bc):
+            write(jnp.int32(i), j).wait()
 
 
 def solution(mesh):
@@ -329,7 +343,7 @@
         rows = -(-bc // 8) * 8
         smem = pl.BlockSpec(memory_space=pltpu.SMEM)
         vmem, hbm = pl.BlockSpec(memory_space=pltpu.VMEM), pl.BlockSpec(memory_space=pl.ANY)
-        n_sem = (n_seq + 48) * CHUNKS
+        n_sem = (n_seq + 56) * CHUNKS
         ysa, ysb, mix = pl.pallas_call(
             functools.partial(exchange_kernel, dims, PLAN),
             in_specs=[hbm, smem, smem, vmem, hbm, hbm, vmem, vmem],
@@ -375,7 +389,7 @@
             out_shape=jax.ShapeDtypeStruct(tokens.shape, tokens.dtype),
             scratch_shapes=[
                 pltpu.VMEM((OUT_BUFS, bc, toks, dim), bf16),
-                pltpu.SemaphoreType.DMA((OUT_BUFS,)),
+                pltpu.SemaphoreType.DMA((OUT_BUFS, bc)),
             ],
             compiler_params=pltpu.CompilerParams(vmem_limit_bytes=COMBINE_VMEM),
             name="combine",

time: 119 us -> 117 us (0.983)
  Pallas kernels: 118 us -> 116 us
    pallas_call x1, Pallas kernels: 100 us -> 98.3 us  [local_layer(): pl.pallas_call(functools.partial(exchange_kernel, dims, PLAN), in_specs=[...]
where the time goes in v4:
time: 117 us
  Pallas kernels  116 us (99%)
    pallas_call x1, Pallas kernels, local_layer(): pl.pallas_call(functools.partial(exchange_kernel, dims, PLAN), in_specs=[...  98.3 us
    pallas_call x1, Pallas kernels, local_layer(): pl.pallas_call(functools.partial(combine_kernel, dims), in_specs=[vmem, s...  18.2 us

profile of v4, /device:TPU:97, one launch (start us, length us, event | category | flops | bytes accessed | tf_op | source)
XLA Modules:
  0.0 117.3 jit_solution(775740820432789802)
XLA Ops:
  0.7 0.0 copy-start
  0.7 98.3 %exchange.1 = (bf16[4,4,2,4,2,16,768]{6,5,4,3,2,1,0:T(8,128)(2,1)S(1)}, bf16[4,4,2,4,2,16,768]{6,5,4,3,2,1,0:T(8,128)(2,1)S(1)}, bf16[64,512,128]{2,1,0:T(8,128)(2,1)S(1)}) custom-call(bf16[64,512,768]{2,1,0:T(8,128)(2,1)} %tok_hbm.1, s32[64]{0:T(128)} %len_ref.3, f32[1]{0:T(128)} %bitcast.1.g_ref, bf16[768,128]{1,0:T(8,128)(2,1)} %phi_ref.1, ...), custom_call_target="tpu_custom_call" | custom-call | tf_op jit(solution)/shard_map/exchange/pallas_call | solution.py:347
  99.0 0.0 copy-done
  99.0 18.2 %combine.1 = bf16[64,512,768]{2,1,0:T(8,128)(2,1)} custom-call(bf16[64,512,128]{2,1,0:T(8,128)(2,1)S(1)} %get-tuple-element.8.mix, s32[64]{0:T(128)S(1)} %copy-done, bf16[4,4,2,4,2,16,768]{6,5,4,3,2,1,0:T(8,128)(2,1)S(1)} %get-tuple-element.9.ysa, bf16[4,4,2,4,2,16,768]{6,5,4,3,2,1,0:T(8,128)(2,1)S(1)} %get-tuple-element.10.ysb), custom_call_target="tpu_custom_call" | custom-call | tf_op jit(solution)/shard_map/combine/pallas_call | solution.py:385
Async XLA Ops:
  0.7 98.3 %copy-start = (s32[64]{0:T(128)S(1)}, s32[64]{0:T(128)}, u32[]{:S(2)}) copy-start(s32[64]{0:T(128)} %len_ref.3) | copy-start | bytes 772
